TPU v7x, 32 devices: a whole 2x2x4 slice. The times are simulated.
32 devices in a mesh: snap: 2 (over y), row: 8 (over z, x), col: 2 (over core).
Axes of the slice: x: 2, y: 2, z: 4, core: 2. Of those that a mesh axis runs over, the one named last changes fastest.
Arguments:
- density: bfloat16 [8192, 1024], P(('snap', 'row'), 'col'), parts along dimension 0, may hold values from -0.5 to 2
- pattern: int32 [256, 32], P(('snap', 'row'), 'col'), parts along dimension 0, may hold values 0 or 1
- filter_mask: int32 [256, 32], P(('snap', 'row')), parts along dimension 0, may hold values 0 or 1
Outputs:
- purified: bfloat16 [8192, 1024], P(('snap', 'row'), 'col'), parts along dimension 0
- traces: float32 [4], P('snap'), parts along dimension 0
There are 2 independent parts, one for each index of `snap`. A program takes and returns all parts, laid end to end along the dimension named above; each array names one. Nothing has to cross between parts.
All inputs are finite; a program needn't handle non-finite values. No bound on the sum of `pattern` or of `filter_mask` on one device may be relied on, other than what follows from the above.
Results may differ from a plain program's by a relative error of at most 0.006.
Values may be sent and summed in bfloat16 or wider, within the bound.
A program may use at most 64 MiB of HBM per device.

v0:
```python
import jax
import jax.numpy as jnp
from jax import lax
from jax.sharding import PartitionSpec as P

BLK = 32


def extended_2(value, sides, width):
    for axis, dim in sides:
        size, length = (lax.axis_size(axis), value.shape[dim])
        up = [(i, (i + 1) % size) for i in range(size - 1)]
        down = [(j, i) for i, j in up]
        last = lax.slice_in_dim(value, length - width, length, axis=dim)
        leading = lax.slice_in_dim(value, 0, width, axis=dim)
        before = lax.ppermute(last, axis, up)
        after = lax.ppermute(leading, axis, down)
        value = jnp.concatenate([before, value, after], axis=dim)
    return value


def valid_slots(first_row, row_count, first_slot, slot_count, half_band, block_total):
    row_index = first_row + jnp.arange(row_count, dtype=jnp.int32)
    slot_index = first_slot + jnp.arange(slot_count, dtype=jnp.int32)
    column_index = row_index[:, None] + slot_index[None, :] - half_band
    return ((column_index >= 0) & (column_index < block_total)).astype(jnp.int32)


def expand_mask(values, keep_mask):
    block_rows = keep_mask.shape[0]
    slot_count = keep_mask.shape[1]
    blocks = values.reshape(block_rows, BLK, slot_count, BLK)
    blocks = blocks * keep_mask.astype(values.dtype)[:, None, :, None]
    return blocks.reshape(block_rows * BLK, slot_count * BLK)


def shift_slots(segment, moved):
    height = segment.shape[0]
    if moved > 0:
        return jnp.concatenate(
            [
                jnp.zeros((height, moved * BLK), segment.dtype),
                segment[:, : segment.shape[1] - moved * BLK],
            ],
            1,
        )
    if moved < 0:
        return jnp.concatenate(
            [segment[:, -moved * BLK :], jnp.zeros((height, -moved * BLK), segment.dtype)], 1
        )
    return segment


def band_part(left, extended, first_slot, column_slots, slot_count, half_band):
    block_rows = left.shape[0] // BLK
    byte_limit = 4 * 1024 * 1024
    group_rows = 1
    for candidate in (8, 4, 2):
        if (
            block_rows % candidate == 0
            and candidate * slot_count * BLK * column_slots * BLK * 2 <= byte_limit
        ):
            group_rows = candidate
            break

    def one_group(group):
        first = group * group_rows
        stacked = []
        for offset in range(slot_count):
            segment = lax.dynamic_slice_in_dim(
                extended, (first + offset) * BLK, group_rows * BLK, 0
            )
            segment = shift_slots(segment, offset - half_band)
            segment = lax.dynamic_slice_in_dim(segment, first_slot * BLK, column_slots * BLK, 1)
            stacked.append(segment.reshape(group_rows, BLK, column_slots * BLK))
        gathered = jnp.stack(stacked, 1).reshape(group_rows, slot_count * BLK, column_slots * BLK)
        left_rows = lax.dynamic_slice_in_dim(left, first * BLK, group_rows * BLK, 0).reshape(
            group_rows, BLK, slot_count * BLK
        )
        result = jnp.einsum("gak,gkn->gan", left_rows, gathered, preferred_element_type=jnp.float32)
        return result.reshape(group_rows * BLK, column_slots * BLK)

    result = lax.map(one_group, jnp.arange(block_rows // group_rows, dtype=jnp.int32))
    return result.reshape(block_rows * BLK, column_slots * BLK)


def diagonal_sum(values, chosen):
    block_rows = values.shape[0] // BLK
    slot_total = values.shape[1] // BLK
    diagonal = jnp.diagonal(values.reshape(block_rows, BLK, slot_total, BLK), axis1=1, axis2=3)
    return jnp.sum(diagonal.astype(jnp.float32) * chosen[None, :, None])


def slot_products(
    full_rows, extended, own_filter, first_slot, half_slots, slot_count, half_band, collect
):
    square = band_part(full_rows, extended, first_slot, half_slots, slot_count, half_band)
    squared = expand_mask(square, own_filter).astype(jnp.bfloat16)
    squared_rows = collect(squared)
    cube = band_part(squared_rows, extended, first_slot, half_slots, slot_count, half_band)
    purified = (3.0 * squared.astype(jnp.float32) - 2.0 * expand_mask(cube, own_filter)).astype(
        jnp.bfloat16
    )
    return (purified, squared)


def per_device(density, pattern, filter_mask):
    half_slots = density.shape[1] // BLK
    slot_count = 2 * half_slots
    block_rows = density.shape[0] // BLK
    col_id = lax.axis_index("col")
    row_id = lax.axis_index("row")
    block_total = block_rows * lax.axis_size("row")
    first_slot = col_id * half_slots
    own_valid = valid_slots(
        row_id * block_rows, block_rows, first_slot, half_slots, half_slots, block_total
    )
    kept = expand_mask(density, pattern * own_valid)
    chosen = (first_slot + jnp.arange(half_slots, dtype=jnp.int32) == half_slots).astype(
        jnp.float32
    )
    trace_kept = diagonal_sum(kept, chosen)
    total_kept = lax.psum(trace_kept, ("row", "col"))
    own_filter = lax.dynamic_slice_in_dim(filter_mask, first_slot, half_slots, 1) * own_valid
    rim_rows = extended_2(kept, (("row", 0),), half_slots * BLK)
    extended = lax.all_gather(rim_rows, "col", axis=1, tiled=True)
    full_rows = extended[half_slots * BLK : half_slots * BLK + block_rows * BLK]

    def collect_half(squared):
        return lax.all_gather(squared, "col", axis=1, tiled=True)

    purified, squared = slot_products(
        full_rows,
        extended,
        own_filter,
        first_slot,
        half_slots,
        slot_count,
        half_slots,
        collect_half,
    )
    trace_squared = diagonal_sum(squared, chosen)
    total_squared = lax.psum(trace_squared, ("row", "col"))
    order_total = block_total * BLK
    traces = jnp.stack([total_kept, total_squared]) / order_total
    return (purified, traces)


def solution(mesh):
    return jax.shard_map(
        per_device,
        mesh=mesh,
        in_specs=(P(("snap", "row"), "col"), P(("snap", "row"), "col"), P(("snap", "row"), None)),
        out_specs=(P(("snap", "row"), "col"), P("snap")),
        check_vma=False,
    )
```

profile of v0, /device:TPU:0, one launch (start us, length us, event | category | flops | bytes accessed | tf_op | source)
XLA Modules:
  0.0 517.6 jit_solution(5589783563380693730)
XLA Ops:
  8.4 2.1 mul.804
  10.6 4.9 collective-permute-start
  15.5 1.3 collective-permute-start.1
  16.8 21.1 %collective-permute-done = bf16[512,512]{1,0:T(8,128)(2,1)S(1)} collective-permute-done((bf16[512,512]{1,0:T(8,128)(2,1)S(1)}, bf16[512,512]{1,0:T(8,128)(2,1)S(1)}, u32[]{:S(2)}, u32[]{:S(2)}) %collective-permute-start) | collective-permute-done | bytes 524320 | tf_op jit(solution)/shard_map/ppermute | solution.py:16
  37.9 1.3 pad_maximum_fusion
  39.2 1.2 reshape.769
  40.5 4.3 copy.7
  44.8 2.4 mul.808.clone
  47.2 4.7 mul.809
  51.9 1.8 all-gather.3.cloned.1.call-done
  53.7 2.3 slice.442
  56.0 1.1 broadcast.199.clone
  57.1 199.7 %while.26 = (s32[]{:T(128)}, f32[4,128,512]{2,1,0:T(8,128)}, s32[4]{0:T(128)S(1)}, bf16[512,1024]{1,0:T(8,128)(2,1)}, bf16[1536,1024]{1,0:T(8,128)(2,1)}, /*inde...) while((s32[]{:T(128)}, f32[4,128,512]{2,1,0:T(8,128)}, ...), condition=%wide.region_1.2_spmd, body=%wide.region_0.1_spmd.sunk | while | flops 134217904 | bytes 56200764 | solution.py:83
  58.6 1.7 constant_dynamic-slice_fusion.65
  60.3 1.7 constant_dynamic-slice_fusion.66
  63.5 1.1 fusion.26
  65.3 1.6 constant_dynamic-update-slice_fusion.129
  66.9 1.6 constant_dynamic-update-slice_fusion.130
  68.4 1.7 constant_dynamic-slice_fusion.67
  103.3 3.0 fusion.27
  108.6 1.7 constant_dynamic-slice_fusion.65
  110.3 1.7 constant_dynamic-slice_fusion.66
  113.4 1.1 fusion.26
  115.2 1.6 constant_dynamic-update-slice_fusion.129
  116.8 1.6 constant_dynamic-update-slice_fusion.130
  118.3 1.7 constant_dynamic-slice_fusion.67
  153.2 3.0 fusion.27
  158.5 1.7 constant_dynamic-slice_fusion.65
  160.2 1.7 constant_dynamic-slice_fusion.66
  163.3 1.1 fusion.26
  165.1 1.6 constant_dynamic-update-slice_fusion.129
  166.7 1.6 constant_dynamic-update-slice_fusion.130
  168.3 1.7 constant_dynamic-slice_fusion.67
  203.1 3.0 fusion.27
  208.4 1.7 constant_dynamic-slice_fusion.65
  210.1 1.7 constant_dynamic-slice_fusion.66
  213.2 1.1 fusion.26
  215.0 1.6 constant_dynamic-update-slice_fusion.129
  216.6 1.6 constant_dynamic-update-slice_fusion.130
  218.2 1.7 constant_dynamic-slice_fusion.67
  253.0 3.0 fusion.27
  256.7 2.5 fusion.4
  259.2 4.6 multiply_bitcast_fusion
  263.8 2.8 gather_fusion
  266.7 2.7 reshape_reshape.10
  269.4 7.3 %copy.8 = f32[16,32,16,32]{2,0,3,1:T(8,128)} copy(f32[16,32,16,32]{3,2,1,0:T(8,128)} %reshape_reshape.10) | data formatting | bytes 2097152 | tf_op jit(solution)/shard_map/reshape;reshape | solution.py:32
  276.6 6.8 %fusion = bf16[16,16,32,32]{1,0,3,2:T(8,128)(2,1)} fusion(f32[16,32,16,32]{2,0,3,1:T(8,128)} %copy.8, f32[16,16]{1,0:T(8,128)S(1)} %get-tuple-element.403), kind=kLoop, calls=%fused_computation.163 | loop fusion | flops 524288 | bytes 1573888 | tf_op jit(solution)/shard_map/jit(diagonal)/transpose | solution.py:90
  283.4 2.8 gather_fusion.1
  287.0 34.8 %all-reduce.62 = (f32[1]{0:T(128)}, f32[1]{0:T(128)}) all-reduce(f32[1]{0:T(128)} %bitcast.140, f32[1]{0:T(128)} %bitcast.138), channel_id=1, replica_groups=mesh['snap'=2,'row'=8,'col'=2] {'row','col'}, use_global_device_ids=true, to_apply=%region_7.8 | all-reduce | flops 2 | bytes 16 | tf_op jit(solution)/shard_map/psum | solution.py:143
  321.9 1.8 maximum_multiply_fusion
  324.8 183.3 %while.27 = (s32[]{:T(128)}, f32[4,128,512]{2,1,0:T(8,128)}, s32[4]{0:T(128)S(1)}, bf16[512,1024]{1,0:T(8,128)(2,1)}, bf16[1536,1024]{1,0:T(8,128)(2,1)S(1)}, /*...) while((s32[]{:T(128)}, f32[4,128,512]{2,1,0:T(8,128)}, ...), condition=%wide.region_3.4_spmd, body=%wide.region_2.3_spmd.sunk | while | flops 134217904 | bytes 43617860 | solution.py:83
  329.9 1.6 constant_dynamic-update-slice_fusion.161
  331.5 1.6 constant_dynamic-update-slice_fusion.162
  366.9 3.0 fusion.31
  375.7 1.6 constant_dynamic-update-slice_fusion.161
  377.3 1.6 constant_dynamic-update-slice_fusion.162
  412.7 3.0 fusion.31
  421.5 1.6 constant_dynamic-update-slice_fusion.161
  423.1 1.6 constant_dynamic-update-slice_fusion.162
  458.5 3.0 fusion.31
  467.3 1.6 constant_dynamic-update-slice_fusion.161
  468.9 1.6 constant_dynamic-update-slice_fusion.162
  504.3 3.0 fusion.31
  508.0 2.8 fusion.3
  (694 shorter events, 299.2 us)
Async XLA Ops:
  7.2 46.5 %all-gather.3.cloned.1.call-start = ((), (), s32[]{:S(2)}) async-start(), calls=%async_computation | async-start | bytes 4718592 | tf_op jit(solution)/shard_map/all_gather | solution.py:126
  10.6 27.3 %collective-permute-start = (bf16[512,512]{1,0:T(8,128)(2,1)S(1)}, bf16[512,512]{1,0:T(8,128)(2,1)S(1)}, u32[]{:S(2)}, u32[]{:S(2)}) collective-permute-start(bf16[512,512]{1,0:T(8,128)(2,1)S(1)} %mul.805), channel_id=1, source_target_pairs={{0,2},{2,4},{4,6},{6,8},{8,10},{10,12},{12,14},{1,3},{3,5},{5,7},{... | collective-permute-start | bytes 1572872 | tf_op jit(solution)/shard_map/ppermute | solution.py:16
  15.5 22.4 %collective-permute-start.1 = (bf16[512,512]{1,0:T(8,128)(2,1)S(1)}, bf16[512,512]{1,0:T(8,128)(2,1)S(1)}, u32[]{:S(2)}, u32[]{:S(2)}) collective-permute-start(bf16[512,512]{1,0:T(8,128)(2,1)S(1)} %mul.805), channel_id=1, source_target_pairs={{2,0},{4,2},{6,4},{8,6},{10,8},{12,10},{14,12},{3,1},{5,3},{7,5},{... | collective-permute-start | bytes 1572872 | tf_op jit(solution)/shard_map/ppermute | solution.py:17
  39.2 284.5 %all-gather.5.cloned.1.call-start = ((), (), s32[]{:S(2)}) async-start(), calls=%async_computation.1 | async-start | bytes 1572864 | tf_op jit(solution)/shard_map/all_gather | solution.py:130
  57.1 13.0 %copy-start = (bf16[1536,1024]{1,0:T(8,128)(2,1)S(1)}, bf16[1536,1024]{1,0:T(8,128)(2,1)}, u32[]{:S(2)}) copy-start(bf16[1536,1024]{1,0:T(8,128)(2,1)} %get-tuple-element.866) | copy-start | bytes 9437188 | tf_op jit(solution)/shard_map/while
  87.8 8.6 %copy-start.10 = (bf16[128,768]{1,0:T(8,128)(2,1)S(1)}, bf16[128,768]{1,0:T(8,128)(2,1)}, u32[]{:S(2)}) copy-start(bf16[128,768]{1,0:T(8,128)(2,1)} %get-tuple-element.656) | copy-start | bytes 589828 | tf_op jit(solution)/shard_map/while
  87.8 8.6 %copy-start.12 = (bf16[128,736]{1,0:T(8,128)(2,1)S(1)}, bf16[128,736]{1,0:T(8,128)(2,1)}, u32[]{:S(2)}) copy-start(bf16[128,736]{1,0:T(8,128)(2,1)} %get-tuple-element.655) | copy-start | bytes 565252 | tf_op jit(solution)/shard_map/while
  87.8 10.0 %copy-start.6 = (bf16[128,704]{1,0:T(8,128)(2,1)S(1)}, bf16[128,704]{1,0:T(8,128)(2,1)}, u32[]{:S(2)}) copy-start(bf16[128,704]{1,0:T(8,128)(2,1)} %get-tuple-element.660) | copy-start | bytes 540676 | tf_op jit(solution)/shard_map/while
  87.8 10.0 %copy-start.8 = (bf16[128,672]{1,0:T(8,128)(2,1)S(1)}, bf16[128,672]{1,0:T(8,128)(2,1)}, u32[]{:S(2)}) copy-start(bf16[128,672]{1,0:T(8,128)(2,1)} %get-tuple-element.659) | copy-start | bytes 516100 | tf_op jit(solution)/shard_map/while
  87.8 11.5 %copy-start.18 = (bf16[128,640]{1,0:T(8,128)(2,1)S(1)}, bf16[128,640]{1,0:T(8,128)(2,1)}, u32[]{:S(2)}) copy-start(bf16[128,640]{1,0:T(8,128)(2,1)} %get-tuple-element.664) | copy-start | bytes 491524 | tf_op jit(solution)/shard_map/while
  87.8 11.5 %copy-start.20 = (bf16[128,608]{1,0:T(8,128)(2,1)S(1)}, bf16[128,608]{1,0:T(8,128)(2,1)}, u32[]{:S(2)}) copy-start(bf16[128,608]{1,0:T(8,128)(2,1)} %get-tuple-element.663) | copy-start | bytes 466948 | tf_op jit(solution)/shard_map/while
  88.1 12.7 %copy-start.14 = (bf16[128,576]{1,0:T(8,128)(2,1)S(1)}, bf16[128,576]{1,0:T(8,128)(2,1)}, u32[]{:S(2)}) copy-start(bf16[128,576]{1,0:T(8,128)(2,1)} %get-tuple-element.668) | copy-start | bytes 442372 | tf_op jit(solution)/shard_map/while
  88.1 12.6 %copy-start.16 = (bf16[128,544]{1,0:T(8,128)(2,1)S(1)}, bf16[128,544]{1,0:T(8,128)(2,1)}, u32[]{:S(2)}) copy-start(bf16[128,544]{1,0:T(8,128)(2,1)} %get-tuple-element.667) | copy-start | bytes 417796 | tf_op jit(solution)/shard_map/while
  107.0 13.0 %copy-start = (bf16[1536,1024]{1,0:T(8,128)(2,1)S(1)}, bf16[1536,1024]{1,0:T(8,128)(2,1)}, u32[]{:S(2)}) copy-start(bf16[1536,1024]{1,0:T(8,128)(2,1)} %get-tuple-element.866) | copy-start | bytes 9437188 | tf_op jit(solution)/shard_map/while
  137.7 8.6 %copy-start.10 = (bf16[128,768]{1,0:T(8,128)(2,1)S(1)}, bf16[128,768]{1,0:T(8,128)(2,1)}, u32[]{:S(2)}) copy-start(bf16[128,768]{1,0:T(8,128)(2,1)} %get-tuple-element.656) | copy-start | bytes 589828 | tf_op jit(solution)/shard_map/while
  137.7 8.6 %copy-start.12 = (bf16[128,736]{1,0:T(8,128)(2,1)S(1)}, bf16[128,736]{1,0:T(8,128)(2,1)}, u32[]{:S(2)}) copy-start(bf16[128,736]{1,0:T(8,128)(2,1)} %get-tuple-element.655) | copy-start | bytes 565252 | tf_op jit(solution)/shard_map/while
  137.7 10.0 %copy-start.6 = (bf16[128,704]{1,0:T(8,128)(2,1)S(1)}, bf16[128,704]{1,0:T(8,128)(2,1)}, u32[]{:S(2)}) copy-start(bf16[128,704]{1,0:T(8,128)(2,1)} %get-tuple-element.660) | copy-start | bytes 540676 | tf_op jit(solution)/shard_map/while
  137.7 10.0 %copy-start.8 = (bf16[128,672]{1,0:T(8,128)(2,1)S(1)}, bf16[128,672]{1,0:T(8,128)(2,1)}, u32[]{:S(2)}) copy-start(bf16[128,672]{1,0:T(8,128)(2,1)} %get-tuple-element.659) | copy-start | bytes 516100 | tf_op jit(solution)/shard_map/while
  137.7 11.5 %copy-start.18 = (bf16[128,640]{1,0:T(8,128)(2,1)S(1)}, bf16[128,640]{1,0:T(8,128)(2,1)}, u32[]{:S(2)}) copy-start(bf16[128,640]{1,0:T(8,128)(2,1)} %get-tuple-element.664) | copy-start | bytes 491524 | tf_op jit(solution)/shard_map/while
  137.8 11.5 %copy-start.20 = (bf16[128,608]{1,0:T(8,128)(2,1)S(1)}, bf16[128,608]{1,0:T(8,128)(2,1)}, u32[]{:S(2)}) copy-start(bf16[128,608]{1,0:T(8,128)(2,1)} %get-tuple-element.663) | copy-start | bytes 466948 | tf_op jit(solution)/shard_map/while
  138.1 12.7 %copy-start.14 = (bf16[128,576]{1,0:T(8,128)(2,1)S(1)}, bf16[128,576]{1,0:T(8,128)(2,1)}, u32[]{:S(2)}) copy-start(bf16[128,576]{1,0:T(8,128)(2,1)} %get-tuple-element.668) | copy-start | bytes 442372 | tf_op jit(solution)/shard_map/while
  138.1 12.6 %copy-start.16 = (bf16[128,544]{1,0:T(8,128)(2,1)S(1)}, bf16[128,544]{1,0:T(8,128)(2,1)}, u32[]{:S(2)}) copy-start(bf16[128,544]{1,0:T(8,128)(2,1)} %get-tuple-element.667) | copy-start | bytes 417796 | tf_op jit(solution)/shard_map/while
  156.9 13.0 %copy-start = (bf16[1536,1024]{1,0:T(8,128)(2,1)S(1)}, bf16[1536,1024]{1,0:T(8,128)(2,1)}, u32[]{:S(2)}) copy-start(bf16[1536,1024]{1,0:T(8,128)(2,1)} %get-tuple-element.866) | copy-start | bytes 9437188 | tf_op jit(solution)/shard_map/while
  187.6 8.6 %copy-start.10 = (bf16[128,768]{1,0:T(8,128)(2,1)S(1)}, bf16[128,768]{1,0:T(8,128)(2,1)}, u32[]{:S(2)}) copy-start(bf16[128,768]{1,0:T(8,128)(2,1)} %get-tuple-element.656) | copy-start | bytes 589828 | tf_op jit(solution)/shard_map/while
  187.6 8.6 %copy-start.12 = (bf16[128,736]{1,0:T(8,128)(2,1)S(1)}, bf16[128,736]{1,0:T(8,128)(2,1)}, u32[]{:S(2)}) copy-start(bf16[128,736]{1,0:T(8,128)(2,1)} %get-tuple-element.655) | copy-start | bytes 565252 | tf_op jit(solution)/shard_map/while
  187.6 10.0 %copy-start.6 = (bf16[128,704]{1,0:T(8,128)(2,1)S(1)}, bf16[128,704]{1,0:T(8,128)(2,1)}, u32[]{:S(2)}) copy-start(bf16[128,704]{1,0:T(8,128)(2,1)} %get-tuple-element.660) | copy-start | bytes 540676 | tf_op jit(solution)/shard_map/while
  187.6 10.0 %copy-start.8 = (bf16[128,672]{1,0:T(8,128)(2,1)S(1)}, bf16[128,672]{1,0:T(8,128)(2,1)}, u32[]{:S(2)}) copy-start(bf16[128,672]{1,0:T(8,128)(2,1)} %get-tuple-element.659) | copy-start | bytes 516100 | tf_op jit(solution)/shard_map/while
  187.7 11.5 %copy-start.18 = (bf16[128,640]{1,0:T(8,128)(2,1)S(1)}, bf16[128,640]{1,0:T(8,128)(2,1)}, u32[]{:S(2)}) copy-start(bf16[128,640]{1,0:T(8,128)(2,1)} %get-tuple-element.664) | copy-start | bytes 491524 | tf_op jit(solution)/shard_map/while
  187.7 11.5 %copy-start.20 = (bf16[128,608]{1,0:T(8,128)(2,1)S(1)}, bf16[128,608]{1,0:T(8,128)(2,1)}, u32[]{:S(2)}) copy-start(bf16[128,608]{1,0:T(8,128)(2,1)} %get-tuple-element.663) | copy-start | bytes 466948 | tf_op jit(solution)/shard_map/while
  188.0 12.7 %copy-start.14 = (bf16[128,576]{1,0:T(8,128)(2,1)S(1)}, bf16[128,576]{1,0:T(8,128)(2,1)}, u32[]{:S(2)}) copy-start(bf16[128,576]{1,0:T(8,128)(2,1)} %get-tuple-element.668) | copy-start | bytes 442372 | tf_op jit(solution)/shard_map/while
  188.0 12.6 %copy-start.16 = (bf16[128,544]{1,0:T(8,128)(2,1)S(1)}, bf16[128,544]{1,0:T(8,128)(2,1)}, u32[]{:S(2)}) copy-start(bf16[128,544]{1,0:T(8,128)(2,1)} %get-tuple-element.667) | copy-start | bytes 417796 | tf_op jit(solution)/shard_map/while
  206.8 13.0 %copy-start = (bf16[1536,1024]{1,0:T(8,128)(2,1)S(1)}, bf16[1536,1024]{1,0:T(8,128)(2,1)}, u32[]{:S(2)}) copy-start(bf16[1536,1024]{1,0:T(8,128)(2,1)} %get-tuple-element.866) | copy-start | bytes 9437188 | tf_op jit(solution)/shard_map/while
  237.5 8.6 %copy-start.12 = (bf16[128,736]{1,0:T(8,128)(2,1)S(1)}, bf16[128,736]{1,0:T(8,128)(2,1)}, u32[]{:S(2)}) copy-start(bf16[128,736]{1,0:T(8,128)(2,1)} %get-tuple-element.655) | copy-start | bytes 565252 | tf_op jit(solution)/shard_map/while
  237.5 10.0 %copy-start.6 = (bf16[128,704]{1,0:T(8,128)(2,1)S(1)}, bf16[128,704]{1,0:T(8,128)(2,1)}, u32[]{:S(2)}) copy-start(bf16[128,704]{1,0:T(8,128)(2,1)} %get-tuple-element.660) | copy-start | bytes 540676 | tf_op jit(solution)/shard_map/while
  237.6 10.0 %copy-start.8 = (bf16[128,672]{1,0:T(8,128)(2,1)S(1)}, bf16[128,672]{1,0:T(8,128)(2,1)}, u32[]{:S(2)}) copy-start(bf16[128,672]{1,0:T(8,128)(2,1)} %get-tuple-element.659) | copy-start | bytes 516100 | tf_op jit(solution)/shard_map/while
  237.6 11.5 %copy-start.18 = (bf16[128,640]{1,0:T(8,128)(2,1)S(1)}, bf16[128,640]{1,0:T(8,128)(2,1)}, u32[]{:S(2)}) copy-start(bf16[128,640]{1,0:T(8,128)(2,1)} %get-tuple-element.664) | copy-start | bytes 491524 | tf_op jit(solution)/shard_map/while
  237.6 11.5 %copy-start.20 = (bf16[128,608]{1,0:T(8,128)(2,1)S(1)}, bf16[128,608]{1,0:T(8,128)(2,1)}, u32[]{:S(2)}) copy-start(bf16[128,608]{1,0:T(8,128)(2,1)} %get-tuple-element.663) | copy-start | bytes 466948 | tf_op jit(solution)/shard_map/while
  237.9 12.7 %copy-start.14 = (bf16[128,576]{1,0:T(8,128)(2,1)S(1)}, bf16[128,576]{1,0:T(8,128)(2,1)}, u32[]{:S(2)}) copy-start(bf16[128,576]{1,0:T(8,128)(2,1)} %get-tuple-element.668) | copy-start | bytes 442372 | tf_op jit(solution)/shard_map/while
  237.9 12.6 %copy-start.16 = (bf16[128,544]{1,0:T(8,128)(2,1)S(1)}, bf16[128,544]{1,0:T(8,128)(2,1)}, u32[]{:S(2)}) copy-start(bf16[128,544]{1,0:T(8,128)(2,1)} %get-tuple-element.667) | copy-start | bytes 417796 | tf_op jit(solution)/shard_map/while
  276.6 48.1 %copy-start.1 = (bf16[1536,1024]{1,0:T(8,128)(2,1)S(1)}, bf16[1536,1024]{1,0:T(8,128)(2,1)}, u32[]{:S(2)}) copy-start(bf16[1536,1024]{1,0:T(8,128)(2,1)} %get-tuple-element.1109) | copy-start | bytes 9437188
  351.4 10.0 %copy-start.7 = (bf16[128,704]{1,0:T(8,128)(2,1)S(1)}, bf16[128,704]{1,0:T(8,128)(2,1)}, u32[]{:S(2)}) copy-start(bf16[128,704]{1,0:T(8,128)(2,1)} %get-tuple-element.729) | copy-start | bytes 540676 | tf_op jit(solution)/shard_map/while
  351.4 10.0 %copy-start.9 = (bf16[128,672]{1,0:T(8,128)(2,1)S(1)}, bf16[128,672]{1,0:T(8,128)(2,1)}, u32[]{:S(2)}) copy-start(bf16[128,672]{1,0:T(8,128)(2,1)} %get-tuple-element.728) | copy-start | bytes 516100 | tf_op jit(solution)/shard_map/while
  351.4 11.5 %copy-start.19 = (bf16[128,640]{1,0:T(8,128)(2,1)S(1)}, bf16[128,640]{1,0:T(8,128)(2,1)}, u32[]{:S(2)}) copy-start(bf16[128,640]{1,0:T(8,128)(2,1)} %get-tuple-element.733) | copy-start | bytes 491524 | tf_op jit(solution)/shard_map/while
  351.4 11.5 %copy-start.21 = (bf16[128,608]{1,0:T(8,128)(2,1)S(1)}, bf16[128,608]{1,0:T(8,128)(2,1)}, u32[]{:S(2)}) copy-start(bf16[128,608]{1,0:T(8,128)(2,1)} %get-tuple-element.732) | copy-start | bytes 466948 | tf_op jit(solution)/shard_map/while
  351.7 12.6 %copy-start.15 = (bf16[128,576]{1,0:T(8,128)(2,1)S(1)}, bf16[128,576]{1,0:T(8,128)(2,1)}, u32[]{:S(2)}) copy-start(bf16[128,576]{1,0:T(8,128)(2,1)} %get-tuple-element.737) | copy-start | bytes 442372 | tf_op jit(solution)/shard_map/while
  351.7 12.6 %copy-start.17 = (bf16[128,544]{1,0:T(8,128)(2,1)S(1)}, bf16[128,544]{1,0:T(8,128)(2,1)}, u32[]{:S(2)}) copy-start(bf16[128,544]{1,0:T(8,128)(2,1)} %get-tuple-element.736) | copy-start | bytes 417796 | tf_op jit(solution)/shard_map/while
  397.2 10.0 %copy-start.7 = (bf16[128,704]{1,0:T(8,128)(2,1)S(1)}, bf16[128,704]{1,0:T(8,128)(2,1)}, u32[]{:S(2)}) copy-start(bf16[128,704]{1,0:T(8,128)(2,1)} %get-tuple-element.729) | copy-start | bytes 540676 | tf_op jit(solution)/shard_map/while
  397.2 10.0 %copy-start.9 = (bf16[128,672]{1,0:T(8,128)(2,1)S(1)}, bf16[128,672]{1,0:T(8,128)(2,1)}, u32[]{:S(2)}) copy-start(bf16[128,672]{1,0:T(8,128)(2,1)} %get-tuple-element.728) | copy-start | bytes 516100 | tf_op jit(solution)/shard_map/while
  397.2 11.5 %copy-start.19 = (bf16[128,640]{1,0:T(8,128)(2,1)S(1)}, bf16[128,640]{1,0:T(8,128)(2,1)}, u32[]{:S(2)}) copy-start(bf16[128,640]{1,0:T(8,128)(2,1)} %get-tuple-element.733) | copy-start | bytes 491524 | tf_op jit(solution)/shard_map/while
  397.2 11.5 %copy-start.21 = (bf16[128,608]{1,0:T(8,128)(2,1)S(1)}, bf16[128,608]{1,0:T(8,128)(2,1)}, u32[]{:S(2)}) copy-start(bf16[128,608]{1,0:T(8,128)(2,1)} %get-tuple-element.732) | copy-start | bytes 466948 | tf_op jit(solution)/shard_map/while
  397.6 12.6 %copy-start.15 = (bf16[128,576]{1,0:T(8,128)(2,1)S(1)}, bf16[128,576]{1,0:T(8,128)(2,1)}, u32[]{:S(2)}) copy-start(bf16[128,576]{1,0:T(8,128)(2,1)} %get-tuple-element.737) | copy-start | bytes 442372 | tf_op jit(solution)/shard_map/while
  397.6 12.6 %copy-start.17 = (bf16[128,544]{1,0:T(8,128)(2,1)S(1)}, bf16[128,544]{1,0:T(8,128)(2,1)}, u32[]{:S(2)}) copy-start(bf16[128,544]{1,0:T(8,128)(2,1)} %get-tuple-element.736) | copy-start | bytes 417796 | tf_op jit(solution)/shard_map/while
  443.0 10.0 %copy-start.7 = (bf16[128,704]{1,0:T(8,128)(2,1)S(1)}, bf16[128,704]{1,0:T(8,128)(2,1)}, u32[]{:S(2)}) copy-start(bf16[128,704]{1,0:T(8,128)(2,1)} %get-tuple-element.729) | copy-start | bytes 540676 | tf_op jit(solution)/shard_map/while
  443.0 10.0 %copy-start.9 = (bf16[128,672]{1,0:T(8,128)(2,1)S(1)}, bf16[128,672]{1,0:T(8,128)(2,1)}, u32[]{:S(2)}) copy-start(bf16[128,672]{1,0:T(8,128)(2,1)} %get-tuple-element.728) | copy-start | bytes 516100 | tf_op jit(solution)/shard_map/while
  443.1 11.5 %copy-start.19 = (bf16[128,640]{1,0:T(8,128)(2,1)S(1)}, bf16[128,640]{1,0:T(8,128)(2,1)}, u32[]{:S(2)}) copy-start(bf16[128,640]{1,0:T(8,128)(2,1)} %get-tuple-element.733) | copy-start | bytes 491524 | tf_op jit(solution)/shard_map/while
  443.1 11.5 %copy-start.21 = (bf16[128,608]{1,0:T(8,128)(2,1)S(1)}, bf16[128,608]{1,0:T(8,128)(2,1)}, u32[]{:S(2)}) copy-start(bf16[128,608]{1,0:T(8,128)(2,1)} %get-tuple-element.732) | copy-start | bytes 466948 | tf_op jit(solution)/shard_map/while
  443.4 12.6 %copy-start.15 = (bf16[128,576]{1,0:T(8,128)(2,1)S(1)}, bf16[128,576]{1,0:T(8,128)(2,1)}, u32[]{:S(2)}) copy-start(bf16[128,576]{1,0:T(8,128)(2,1)} %get-tuple-element.737) | copy-start | bytes 442372 | tf_op jit(solution)/shard_map/while
  443.4 12.6 %copy-start.17 = (bf16[128,544]{1,0:T(8,128)(2,1)S(1)}, bf16[128,544]{1,0:T(8,128)(2,1)}, u32[]{:S(2)}) copy-start(bf16[128,544]{1,0:T(8,128)(2,1)} %get-tuple-element.736) | copy-start | bytes 417796 | tf_op jit(solution)/shard_map/while
  488.8 10.0 %copy-start.7 = (bf16[128,704]{1,0:T(8,128)(2,1)S(1)}, bf16[128,704]{1,0:T(8,128)(2,1)}, u32[]{:S(2)}) copy-start(bf16[128,704]{1,0:T(8,128)(2,1)} %get-tuple-element.729) | copy-start | bytes 540676 | tf_op jit(solution)/shard_map/while
  488.9 10.0 %copy-start.9 = (bf16[128,672]{1,0:T(8,128)(2,1)S(1)}, bf16[128,672]{1,0:T(8,128)(2,1)}, u32[]{:S(2)}) copy-start(bf16[128,672]{1,0:T(8,128)(2,1)} %get-tuple-element.728) | copy-start | bytes 516100 | tf_op jit(solution)/shard_map/while
  488.9 11.5 %copy-start.19 = (bf16[128,640]{1,0:T(8,128)(2,1)S(1)}, bf16[128,640]{1,0:T(8,128)(2,1)}, u32[]{:S(2)}) copy-start(bf16[128,640]{1,0:T(8,128)(2,1)} %get-tuple-element.733) | copy-start | bytes 491524 | tf_op jit(solution)/shard_map/while
  488.9 11.5 %copy-start.21 = (bf16[128,608]{1,0:T(8,128)(2,1)S(1)}, bf16[128,608]{1,0:T(8,128)(2,1)}, u32[]{:S(2)}) copy-start(bf16[128,608]{1,0:T(8,128)(2,1)} %get-tuple-element.732) | copy-start | bytes 466948 | tf_op jit(solution)/shard_map/while
  489.2 12.6 %copy-start.15 = (bf16[128,576]{1,0:T(8,128)(2,1)S(1)}, bf16[128,576]{1,0:T(8,128)(2,1)}, u32[]{:S(2)}) copy-start(bf16[128,576]{1,0:T(8,128)(2,1)} %get-tuple-element.737) | copy-start | bytes 442372 | tf_op jit(solution)/shard_map/while
  489.2 12.6 %copy-start.17 = (bf16[128,544]{1,0:T(8,128)(2,1)S(1)}, bf16[128,544]{1,0:T(8,128)(2,1)}, u32[]{:S(2)}) copy-start(bf16[128,544]{1,0:T(8,128)(2,1)} %get-tuple-element.736) | copy-start | bytes 417796 | tf_op jit(solution)/shard_map/while
  (27 other events, 201.9 us)
Sparse Core Ops, SparseCore 0:
  39.3 14.3 all-gather.2
  259.4 10.2 all-gather.4
where the time goes:
time: 520 us; the launch traced here: 518 us
  local copies, waits for them, and re-layouts  381 us (73%)
  blocking collectives  34.8 us (7%)
  matrix products  23.9 us (5%)
  waiting for transfers between devices  22.9 us (4%)
  other arithmetic  21.4 us (4%)
  between operations  14.2 us (3%)
  loops' own time  13.2 us (3%)
  starting transfers between devices  6.27 us (1%)
    while x416, local copies, waits for them, and re-layouts  178 us
    slice x120, local copies, waits for them, and re-layouts, shift_slots(): segment[:, :segment.shape[1] - moved * BLK]  98.7 us
    dynamic_slice x136, local copies, waits for them, and re-layouts, one_group(): lax.dynamic_slice_in_dim(segment, first_slot * BLK, column_slots * BLK, 1)  45.4 us
    psum x1, blocking collectives, per_device(): total_squared = lax.psum(trace_squared, ('row', 'col'))  34.8 us
    dot_general x8, matrix products, one_group(): jnp.einsum('gak,gkn->gan', left_rows, gathered, preferred_element_type=jn...  23.9 us
    ppermute x1, waiting for transfers between devices, extended_2(): before = lax.ppermute(last, axis, up)  21.1 us
    another operation x2, loops' own time, band_part(): lax.map(one_group, jnp.arange(block_rows // group_rows, dtype=jnp.int32))  13.2 us
    transpose x2, other arithmetic, diagonal_sum(): jnp.diagonal(values.reshape(block_rows, BLK, slot_total, BLK), axis1=1, a...  11.4 us
  transfers between devices with their start and end apart: 4, of which 2 were waited for; matrix products, arithmetic and copies ran while one was open for 8% of the time, Pallas kernels for 0%

commit v1 on v0

--- a/solution.py
+++ b/solution.py
@@ -140,7 +140,8 @@
         collect_half,
     )
     trace_squared = diagonal_sum(squared, chosen)
-    total_squared = lax.psum(trace_squared, ("row", "col"))
+    parts = lax.all_gather(trace_squared, ("row", "col"), axis=0, tiled=False)
+    total_squared = parts.sum(axis=0)
     order_total = block_total * BLK
     traces = jnp.stack([total_kept, total_squared]) / order_total
     return (purified, traces)

time: 520 us -> 522 us (level)
    psum x1 -> x0, blocking collectives: 34.8 us -> none  [per_device(): total_squared = lax.psum(trace_squared, ('row', 'col'))]
    unnamed x0 -> x1, blocking collectives: none -> 34.8 us
  transfers between devices with their start and end apart: 4 -> 4, of which waited for: 2 -> 2; matrix products, arithmetic and copies ran while one was open for 8% -> 9% of each run, Pallas kernels for 0% -> 0%
where the time goes in v1:
time: 522 us; the launch traced here: 520 us
  local copies, waits for them, and re-layouts  383 us (73%)
  blocking collectives  34.8 us (7%)
  matrix products  23.9 us (5%)
  waiting for transfers between devices  22.9 us (4%)
  other arithmetic  22.1 us (4%)
  between operations  14.2 us (3%)
  loops' own time  12.7 us (2%)
  starting transfers between devices  6.27 us (1%)
    while x416, local copies, waits for them, and re-layouts  178 us
    slice x120, local copies, waits for them, and re-layouts, shift_slots(): segment[:, :segment.shape[1] - moved * BLK]  98.8 us
    dynamic_slice x136, local copies, waits for them, and re-layouts, one_group(): lax.dynamic_slice_in_dim(segment, first_slot * BLK, column_slots * BLK, 1)  45.4 us
    unnamed x1, blocking collectives  34.8 us
    dot_general x8, matrix products, one_group(): jnp.einsum('gak,gkn->gan', left_rows, gathered, preferred_element_type=jn...  23.9 us
    ppermute x1, waiting for transfers between devices, extended_2(): before = lax.ppermute(last, axis, up)  21.1 us
    another operation x2, loops' own time, band_part(): lax.map(one_group, jnp.arange(block_rows // group_rows, dtype=jnp.int32))  12.7 us
    transpose x2, other arithmetic, diagonal_sum(): jnp.diagonal(values.reshape(block_rows, BLK, slot_total, BLK), axis1=1, a...  11.4 us
  transfers between devices with their start and end apart: 4, of which 2 were waited for; matrix products, arithmetic and copies ran while one was open for 9% of the time, Pallas kernels for 0%

profile of v1, /device:TPU:0, one launch (start us, length us, event | category | flops | bytes accessed | tf_op | source)
XLA Modules:
  0.0 519.9 jit_solution(238078020381052510)
XLA Ops:
  8.4 2.1 mul.804
  10.6 4.9 collective-permute-start
  15.5 1.3 collective-permute-start.1
  16.8 21.1 %collective-permute-done = bf16[512,512]{1,0:T(8,128)(2,1)S(1)} collective-permute-done((bf16[512,512]{1,0:T(8,128)(2,1)S(1)}, bf16[512,512]{1,0:T(8,128)(2,1)S(1)}, u32[]{:S(2)}, u32[]{:S(2)}) %collective-permute-start) | collective-permute-done | bytes 524320 | tf_op jit(solution)/shard_map/ppermute | solution.py:16
  37.9 1.2 pad_maximum_fusion
  39.2 1.2 reshape.769
  40.5 4.3 copy.7
  44.8 2.4 mul.808.clone
  47.2 4.7 mul.809
  51.9 1.8 all-gather.3.cloned.1.call-done
  53.7 2.3 slice.442
  57.1 199.6 %while.26 = (s32[]{:T(128)}, f32[4,128,512]{2,1,0:T(8,128)}, s32[4]{0:T(128)S(1)}, bf16[512,1024]{1,0:T(8,128)(2,1)}, bf16[1536,1024]{1,0:T(8,128)(2,1)}, /*inde...) while((s32[]{:T(128)}, f32[4,128,512]{2,1,0:T(8,128)}, ...), condition=%wide.region_1.2_spmd, body=%wide.region_0.1_spmd.sunk | while | flops 134217904 | bytes 56200764 | solution.py:83
  58.7 1.7 constant_dynamic-slice_fusion.65
  60.4 1.7 constant_dynamic-slice_fusion.66
  63.5 1.1 fusion.26
  65.3 1.6 constant_dynamic-update-slice_fusion.129
  66.9 1.6 constant_dynamic-update-slice_fusion.130
  68.4 1.7 constant_dynamic-slice_fusion.67
  103.2 3.0 fusion.27
  108.6 1.7 constant_dynamic-slice_fusion.65
  110.3 1.7 constant_dynamic-slice_fusion.66
  113.4 1.1 fusion.26
  115.2 1.6 constant_dynamic-update-slice_fusion.129
  116.8 1.6 constant_dynamic-update-slice_fusion.130
  118.3 1.7 constant_dynamic-slice_fusion.67
  153.1 3.0 fusion.27
  158.5 1.7 constant_dynamic-slice_fusion.65
  160.2 1.7 constant_dynamic-slice_fusion.66
  163.3 1.1 fusion.26
  165.1 1.6 constant_dynamic-update-slice_fusion.129
  166.7 1.6 constant_dynamic-update-slice_fusion.130
  168.3 1.7 constant_dynamic-slice_fusion.67
  203.1 3.0 fusion.27
  208.4 1.7 constant_dynamic-slice_fusion.65
  210.1 1.7 constant_dynamic-slice_fusion.66
  213.2 1.1 fusion.26
  215.0 1.6 constant_dynamic-update-slice_fusion.129
  216.6 1.6 constant_dynamic-update-slice_fusion.130
  218.1 1.7 constant_dynamic-slice_fusion.67
  252.9 3.0 fusion.27
  256.7 2.5 fusion.4
  259.2 4.6 multiply_bitcast_fusion
  263.8 2.8 gather_fusion
  267.3 2.7 reshape_reshape.10
  269.9 7.3 %copy.8 = f32[16,32,16,32]{2,0,3,1:T(8,128)} copy(f32[16,32,16,32]{3,2,1,0:T(8,128)} %reshape_reshape.10) | data formatting | bytes 2097152 | tf_op jit(solution)/shard_map/reshape;reshape | solution.py:32
  277.2 6.8 %fusion = bf16[16,16,32,32]{1,0,3,2:T(8,128)(2,1)} fusion(f32[16,32,16,32]{2,0,3,1:T(8,128)} %copy.8, f32[16,16]{1,0:T(8,128)S(1)} %get-tuple-element.403), kind=kLoop, calls=%fused_computation.163 | loop fusion | flops 524288 | bytes 1573888 | tf_op jit(solution)/shard_map/jit(diagonal)/transpose | solution.py:90
  284.0 2.8 gather_fusion.1
  287.6 1.3 dynamic-update-slice
  288.9 34.8 %all-reduce.63 = (f32[16]{0:T(128)S(1)}, f32[1]{0:T(128)}) all-reduce(f32[16]{0:T(128)S(1)} %dynamic-update-slice, f32[1]{0:T(128)} %bitcast.138), channel_id=1, replica_groups=mesh['snap'=2,'row'=8,'col'=2] {'row','col'}, use_global_device_ids=true, to_apply=%add.62 | all-reduce | flops 17 | bytes 136
  324.4 1.8 maximum_multiply_fusion
  327.3 183.0 %while.27 = (s32[]{:T(128)}, f32[4,128,512]{2,1,0:T(8,128)}, s32[4]{0:T(128)S(1)}, bf16[512,1024]{1,0:T(8,128)(2,1)}, bf16[1536,1024]{1,0:T(8,128)(2,1)S(1)}, /*...) while((s32[]{:T(128)}, f32[4,128,512]{2,1,0:T(8,128)}, ...), condition=%wide.region_3.4_spmd, body=%wide.region_2.3_spmd.sunk | while | flops 134217904 | bytes 43617860 | solution.py:83
  332.3 1.6 constant_dynamic-update-slice_fusion.161
  333.9 1.6 constant_dynamic-update-slice_fusion.162
  369.3 3.0 fusion.31
  378.1 1.6 constant_dynamic-update-slice_fusion.161
  379.6 1.6 constant_dynamic-update-slice_fusion.162
  415.1 3.0 fusion.31
  423.8 1.6 constant_dynamic-update-slice_fusion.161
  425.4 1.6 constant_dynamic-update-slice_fusion.162
  460.8 3.0 fusion.31
  469.5 1.6 constant_dynamic-update-slice_fusion.161
  471.1 1.6 constant_dynamic-update-slice_fusion.162
  506.6 3.0 fusion.31
  510.3 2.8 fusion.3
  (700 shorter events, 301.6 us)
Async XLA Ops:
  7.2 46.5 %all-gather.3.cloned.1.call-start = ((), (), s32[]{:S(2)}) async-start(), calls=%async_computation | async-start | bytes 4718592 | tf_op jit(solution)/shard_map/all_gather | solution.py:126
  10.6 27.3 %collective-permute-start = (bf16[512,512]{1,0:T(8,128)(2,1)S(1)}, bf16[512,512]{1,0:T(8,128)(2,1)S(1)}, u32[]{:S(2)}, u32[]{:S(2)}) collective-permute-start(bf16[512,512]{1,0:T(8,128)(2,1)S(1)} %mul.805), channel_id=1, source_target_pairs={{0,2},{2,4},{4,6},{6,8},{8,10},{10,12},{12,14},{1,3},{3,5},{5,7},{... | collective-permute-start | bytes 1572872 | tf_op jit(solution)/shard_map/ppermute | solution.py:16
  15.5 22.4 %collective-permute-start.1 = (bf16[512,512]{1,0:T(8,128)(2,1)S(1)}, bf16[512,512]{1,0:T(8,128)(2,1)S(1)}, u32[]{:S(2)}, u32[]{:S(2)}) collective-permute-start(bf16[512,512]{1,0:T(8,128)(2,1)S(1)} %mul.805), channel_id=1, source_target_pairs={{2,0},{4,2},{6,4},{8,6},{10,8},{12,10},{14,12},{3,1},{5,3},{7,5},{... | collective-permute-start | bytes 1572872 | tf_op jit(solution)/shard_map/ppermute | solution.py:17
  39.2 287.0 %all-gather.5.cloned.1.call-start = ((), (), s32[]{:S(2)}) async-start(), calls=%async_computation.1 | async-start | bytes 1572864 | tf_op jit(solution)/shard_map/all_gather | solution.py:130
  57.1 13.1 %copy-start = (bf16[1536,1024]{1,0:T(8,128)(2,1)S(1)}, bf16[1536,1024]{1,0:T(8,128)(2,1)}, u32[]{:S(2)}) copy-start(bf16[1536,1024]{1,0:T(8,128)(2,1)} %get-tuple-element.866) | copy-start | bytes 9437188 | tf_op jit(solution)/shard_map/while
  87.8 8.6 %copy-start.10 = (bf16[128,768]{1,0:T(8,128)(2,1)S(1)}, bf16[128,768]{1,0:T(8,128)(2,1)}, u32[]{:S(2)}) copy-start(bf16[128,768]{1,0:T(8,128)(2,1)} %get-tuple-element.656) | copy-start | bytes 589828 | tf_op jit(solution)/shard_map/while
  87.8 8.6 %copy-start.12 = (bf16[128,736]{1,0:T(8,128)(2,1)S(1)}, bf16[128,736]{1,0:T(8,128)(2,1)}, u32[]{:S(2)}) copy-start(bf16[128,736]{1,0:T(8,128)(2,1)} %get-tuple-element.655) | copy-start | bytes 565252 | tf_op jit(solution)/shard_map/while
  87.8 10.0 %copy-start.6 = (bf16[128,704]{1,0:T(8,128)(2,1)S(1)}, bf16[128,704]{1,0:T(8,128)(2,1)}, u32[]{:S(2)}) copy-start(bf16[128,704]{1,0:T(8,128)(2,1)} %get-tuple-element.660) | copy-start | bytes 540676 | tf_op jit(solution)/shard_map/while
  87.8 10.0 %copy-start.8 = (bf16[128,672]{1,0:T(8,128)(2,1)S(1)}, bf16[128,672]{1,0:T(8,128)(2,1)}, u32[]{:S(2)}) copy-start(bf16[128,672]{1,0:T(8,128)(2,1)} %get-tuple-element.659) | copy-start | bytes 516100 | tf_op jit(solution)/shard_map/while
  87.8 11.5 %copy-start.18 = (bf16[128,640]{1,0:T(8,128)(2,1)S(1)}, bf16[128,640]{1,0:T(8,128)(2,1)}, u32[]{:S(2)}) copy-start(bf16[128,640]{1,0:T(8,128)(2,1)} %get-tuple-element.664) | copy-start | bytes 491524 | tf_op jit(solution)/shard_map/while
  87.8 11.5 %copy-start.20 = (bf16[128,608]{1,0:T(8,128)(2,1)S(1)}, bf16[128,608]{1,0:T(8,128)(2,1)}, u32[]{:S(2)}) copy-start(bf16[128,608]{1,0:T(8,128)(2,1)} %get-tuple-element.663) | copy-start | bytes 466948 | tf_op jit(solution)/shard_map/while
  88.1 12.6 %copy-start.14 = (bf16[128,576]{1,0:T(8,128)(2,1)S(1)}, bf16[128,576]{1,0:T(8,128)(2,1)}, u32[]{:S(2)}) copy-start(bf16[128,576]{1,0:T(8,128)(2,1)} %get-tuple-element.668) | copy-start | bytes 442372 | tf_op jit(solution)/shard_map/while
  88.1 12.6 %copy-start.16 = (bf16[128,544]{1,0:T(8,128)(2,1)S(1)}, bf16[128,544]{1,0:T(8,128)(2,1)}, u32[]{:S(2)}) copy-start(bf16[128,544]{1,0:T(8,128)(2,1)} %get-tuple-element.667) | copy-start | bytes 417796 | tf_op jit(solution)/shard_map/while
  107.0 13.1 %copy-start = (bf16[1536,1024]{1,0:T(8,128)(2,1)S(1)}, bf16[1536,1024]{1,0:T(8,128)(2,1)}, u32[]{:S(2)}) copy-start(bf16[1536,1024]{1,0:T(8,128)(2,1)} %get-tuple-element.866) | copy-start | bytes 9437188 | tf_op jit(solution)/shard_map/while
  137.7 8.6 %copy-start.10 = (bf16[128,768]{1,0:T(8,128)(2,1)S(1)}, bf16[128,768]{1,0:T(8,128)(2,1)}, u32[]{:S(2)}) copy-start(bf16[128,768]{1,0:T(8,128)(2,1)} %get-tuple-element.656) | copy-start | bytes 589828 | tf_op jit(solution)/shard_map/while
  137.7 8.6 %copy-start.12 = (bf16[128,736]{1,0:T(8,128)(2,1)S(1)}, bf16[128,736]{1,0:T(8,128)(2,1)}, u32[]{:S(2)}) copy-start(bf16[128,736]{1,0:T(8,128)(2,1)} %get-tuple-element.655) | copy-start | bytes 565252 | tf_op jit(solution)/shard_map/while
  137.7 10.0 %copy-start.6 = (bf16[128,704]{1,0:T(8,128)(2,1)S(1)}, bf16[128,704]{1,0:T(8,128)(2,1)}, u32[]{:S(2)}) copy-start(bf16[128,704]{1,0:T(8,128)(2,1)} %get-tuple-element.660) | copy-start | bytes 540676 | tf_op jit(solution)/shard_map/while
  137.7 10.0 %copy-start.8 = (bf16[128,672]{1,0:T(8,128)(2,1)S(1)}, bf16[128,672]{1,0:T(8,128)(2,1)}, u32[]{:S(2)}) copy-start(bf16[128,672]{1,0:T(8,128)(2,1)} %get-tuple-element.659) | copy-start | bytes 516100 | tf_op jit(solution)/shard_map/while
  137.7 11.5 %copy-start.18 = (bf16[128,640]{1,0:T(8,128)(2,1)S(1)}, bf16[128,640]{1,0:T(8,128)(2,1)}, u32[]{:S(2)}) copy-start(bf16[128,640]{1,0:T(8,128)(2,1)} %get-tuple-element.664) | copy-start | bytes 491524 | tf_op jit(solution)/shard_map/while
  137.7 11.5 %copy-start.20 = (bf16[128,608]{1,0:T(8,128)(2,1)S(1)}, bf16[128,608]{1,0:T(8,128)(2,1)}, u32[]{:S(2)}) copy-start(bf16[128,608]{1,0:T(8,128)(2,1)} %get-tuple-element.663) | copy-start | bytes 466948 | tf_op jit(solution)/shard_map/while
  138.0 12.6 %copy-start.14 = (bf16[128,576]{1,0:T(8,128)(2,1)S(1)}, bf16[128,576]{1,0:T(8,128)(2,1)}, u32[]{:S(2)}) copy-start(bf16[128,576]{1,0:T(8,128)(2,1)} %get-tuple-element.668) | copy-start | bytes 442372 | tf_op jit(solution)/shard_map/while
  138.0 12.6 %copy-start.16 = (bf16[128,544]{1,0:T(8,128)(2,1)S(1)}, bf16[128,544]{1,0:T(8,128)(2,1)}, u32[]{:S(2)}) copy-start(bf16[128,544]{1,0:T(8,128)(2,1)} %get-tuple-element.667) | copy-start | bytes 417796 | tf_op jit(solution)/shard_map/while
  156.9 13.1 %copy-start = (bf16[1536,1024]{1,0:T(8,128)(2,1)S(1)}, bf16[1536,1024]{1,0:T(8,128)(2,1)}, u32[]{:S(2)}) copy-start(bf16[1536,1024]{1,0:T(8,128)(2,1)} %get-tuple-element.866) | copy-start | bytes 9437188 | tf_op jit(solution)/shard_map/while
  187.6 8.6 %copy-start.10 = (bf16[128,768]{1,0:T(8,128)(2,1)S(1)}, bf16[128,768]{1,0:T(8,128)(2,1)}, u32[]{:S(2)}) copy-start(bf16[128,768]{1,0:T(8,128)(2,1)} %get-tuple-element.656) | copy-start | bytes 589828 | tf_op jit(solution)/shard_map/while
  187.6 8.6 %copy-start.12 = (bf16[128,736]{1,0:T(8,128)(2,1)S(1)}, bf16[128,736]{1,0:T(8,128)(2,1)}, u32[]{:S(2)}) copy-start(bf16[128,736]{1,0:T(8,128)(2,1)} %get-tuple-element.655) | copy-start | bytes 565252 | tf_op jit(solution)/shard_map/while
  187.6 10.0 %copy-start.6 = (bf16[128,704]{1,0:T(8,128)(2,1)S(1)}, bf16[128,704]{1,0:T(8,128)(2,1)}, u32[]{:S(2)}) copy-start(bf16[128,704]{1,0:T(8,128)(2,1)} %get-tuple-element.660) | copy-start | bytes 540676 | tf_op jit(solution)/shard_map/while
  187.6 10.0 %copy-start.8 = (bf16[128,672]{1,0:T(8,128)(2,1)S(1)}, bf16[128,672]{1,0:T(8,128)(2,1)}, u32[]{:S(2)}) copy-start(bf16[128,672]{1,0:T(8,128)(2,1)} %get-tuple-element.659) | copy-start | bytes 516100 | tf_op jit(solution)/shard_map/while
  187.6 11.5 %copy-start.18 = (bf16[128,640]{1,0:T(8,128)(2,1)S(1)}, bf16[128,640]{1,0:T(8,128)(2,1)}, u32[]{:S(2)}) copy-start(bf16[128,640]{1,0:T(8,128)(2,1)} %get-tuple-element.664) | copy-start | bytes 491524 | tf_op jit(solution)/shard_map/while
  187.6 11.5 %copy-start.20 = (bf16[128,608]{1,0:T(8,128)(2,1)S(1)}, bf16[128,608]{1,0:T(8,128)(2,1)}, u32[]{:S(2)}) copy-start(bf16[128,608]{1,0:T(8,128)(2,1)} %get-tuple-element.663) | copy-start | bytes 466948 | tf_op jit(solution)/shard_map/while
  187.9 12.6 %copy-start.14 = (bf16[128,576]{1,0:T(8,128)(2,1)S(1)}, bf16[128,576]{1,0:T(8,128)(2,1)}, u32[]{:S(2)}) copy-start(bf16[128,576]{1,0:T(8,128)(2,1)} %get-tuple-element.668) | copy-start | bytes 442372 | tf_op jit(solution)/shard_map/while
  187.9 12.6 %copy-start.16 = (bf16[128,544]{1,0:T(8,128)(2,1)S(1)}, bf16[128,544]{1,0:T(8,128)(2,1)}, u32[]{:S(2)}) copy-start(bf16[128,544]{1,0:T(8,128)(2,1)} %get-tuple-element.667) | copy-start | bytes 417796 | tf_op jit(solution)/shard_map/while
  206.8 13.1 %copy-start = (bf16[1536,1024]{1,0:T(8,128)(2,1)S(1)}, bf16[1536,1024]{1,0:T(8,128)(2,1)}, u32[]{:S(2)}) copy-start(bf16[1536,1024]{1,0:T(8,128)(2,1)} %get-tuple-element.866) | copy-start | bytes 9437188 | tf_op jit(solution)/shard_map/while
  237.5 8.6 %copy-start.12 = (bf16[128,736]{1,0:T(8,128)(2,1)S(1)}, bf16[128,736]{1,0:T(8,128)(2,1)}, u32[]{:S(2)}) copy-start(bf16[128,736]{1,0:T(8,128)(2,1)} %get-tuple-element.655) | copy-start | bytes 565252 | tf_op jit(solution)/shard_map/while
  237.5 10.0 %copy-start.6 = (bf16[128,704]{1,0:T(8,128)(2,1)S(1)}, bf16[128,704]{1,0:T(8,128)(2,1)}, u32[]{:S(2)}) copy-start(bf16[128,704]{1,0:T(8,128)(2,1)} %get-tuple-element.660) | copy-start | bytes 540676 | tf_op jit(solution)/shard_map/while
  237.5 10.0 %copy-start.8 = (bf16[128,672]{1,0:T(8,128)(2,1)S(1)}, bf16[128,672]{1,0:T(8,128)(2,1)}, u32[]{:S(2)}) copy-start(bf16[128,672]{1,0:T(8,128)(2,1)} %get-tuple-element.659) | copy-start | bytes 516100 | tf_op jit(solution)/shard_map/while
  237.5 11.5 %copy-start.18 = (bf16[128,640]{1,0:T(8,128)(2,1)S(1)}, bf16[128,640]{1,0:T(8,128)(2,1)}, u32[]{:S(2)}) copy-start(bf16[128,640]{1,0:T(8,128)(2,1)} %get-tuple-element.664) | copy-start | bytes 491524 | tf_op jit(solution)/shard_map/while
  237.5 11.5 %copy-start.20 = (bf16[128,608]{1,0:T(8,128)(2,1)S(1)}, bf16[128,608]{1,0:T(8,128)(2,1)}, u32[]{:S(2)}) copy-start(bf16[128,608]{1,0:T(8,128)(2,1)} %get-tuple-element.663) | copy-start | bytes 466948 | tf_op jit(solution)/shard_map/while
  237.8 12.6 %copy-start.14 = (bf16[128,576]{1,0:T(8,128)(2,1)S(1)}, bf16[128,576]{1,0:T(8,128)(2,1)}, u32[]{:S(2)}) copy-start(bf16[128,576]{1,0:T(8,128)(2,1)} %get-tuple-element.668) | copy-start | bytes 442372 | tf_op jit(solution)/shard_map/while
  237.8 12.6 %copy-start.16 = (bf16[128,544]{1,0:T(8,128)(2,1)S(1)}, bf16[128,544]{1,0:T(8,128)(2,1)}, u32[]{:S(2)}) copy-start(bf16[128,544]{1,0:T(8,128)(2,1)} %get-tuple-element.667) | copy-start | bytes 417796 | tf_op jit(solution)/shard_map/while
  277.2 50.1 %copy-start.1 = (bf16[1536,1024]{1,0:T(8,128)(2,1)S(1)}, bf16[1536,1024]{1,0:T(8,128)(2,1)}, u32[]{:S(2)}) copy-start(bf16[1536,1024]{1,0:T(8,128)(2,1)} %get-tuple-element.1109) | copy-start | bytes 9437188
  353.9 10.0 %copy-start.7 = (bf16[128,704]{1,0:T(8,128)(2,1)S(1)}, bf16[128,704]{1,0:T(8,128)(2,1)}, u32[]{:S(2)}) copy-start(bf16[128,704]{1,0:T(8,128)(2,1)} %get-tuple-element.729) | copy-start | bytes 540676 | tf_op jit(solution)/shard_map/while
  353.9 10.0 %copy-start.9 = (bf16[128,672]{1,0:T(8,128)(2,1)S(1)}, bf16[128,672]{1,0:T(8,128)(2,1)}, u32[]{:S(2)}) copy-start(bf16[128,672]{1,0:T(8,128)(2,1)} %get-tuple-element.728) | copy-start | bytes 516100 | tf_op jit(solution)/shard_map/while
  353.9 11.5 %copy-start.19 = (bf16[128,640]{1,0:T(8,128)(2,1)S(1)}, bf16[128,640]{1,0:T(8,128)(2,1)}, u32[]{:S(2)}) copy-start(bf16[128,640]{1,0:T(8,128)(2,1)} %get-tuple-element.733) | copy-start | bytes 491524 | tf_op jit(solution)/shard_map/while
  353.9 11.5 %copy-start.21 = (bf16[128,608]{1,0:T(8,128)(2,1)S(1)}, bf16[128,608]{1,0:T(8,128)(2,1)}, u32[]{:S(2)}) copy-start(bf16[128,608]{1,0:T(8,128)(2,1)} %get-tuple-element.732) | copy-start | bytes 466948 | tf_op jit(solution)/shard_map/while
  354.2 12.6 %copy-start.15 = (bf16[128,576]{1,0:T(8,128)(2,1)S(1)}, bf16[128,576]{1,0:T(8,128)(2,1)}, u32[]{:S(2)}) copy-start(bf16[128,576]{1,0:T(8,128)(2,1)} %get-tuple-element.737) | copy-start | bytes 442372 | tf_op jit(solution)/shard_map/while
  354.2 12.6 %copy-start.17 = (bf16[128,544]{1,0:T(8,128)(2,1)S(1)}, bf16[128,544]{1,0:T(8,128)(2,1)}, u32[]{:S(2)}) copy-start(bf16[128,544]{1,0:T(8,128)(2,1)} %get-tuple-element.736) | copy-start | bytes 417796 | tf_op jit(solution)/shard_map/while
  399.6 10.0 %copy-start.7 = (bf16[128,704]{1,0:T(8,128)(2,1)S(1)}, bf16[128,704]{1,0:T(8,128)(2,1)}, u32[]{:S(2)}) copy-start(bf16[128,704]{1,0:T(8,128)(2,1)} %get-tuple-element.729) | copy-start | bytes 540676 | tf_op jit(solution)/shard_map/while
  399.6 10.0 %copy-start.9 = (bf16[128,672]{1,0:T(8,128)(2,1)S(1)}, bf16[128,672]{1,0:T(8,128)(2,1)}, u32[]{:S(2)}) copy-start(bf16[128,672]{1,0:T(8,128)(2,1)} %get-tuple-element.728) | copy-start | bytes 516100 | tf_op jit(solution)/shard_map/while
  399.6 11.5 %copy-start.19 = (bf16[128,640]{1,0:T(8,128)(2,1)S(1)}, bf16[128,640]{1,0:T(8,128)(2,1)}, u32[]{:S(2)}) copy-start(bf16[128,640]{1,0:T(8,128)(2,1)} %get-tuple-element.733) | copy-start | bytes 491524 | tf_op jit(solution)/shard_map/while
  399.7 11.5 %copy-start.21 = (bf16[128,608]{1,0:T(8,128)(2,1)S(1)}, bf16[128,608]{1,0:T(8,128)(2,1)}, u32[]{:S(2)}) copy-start(bf16[128,608]{1,0:T(8,128)(2,1)} %get-tuple-element.732) | copy-start | bytes 466948 | tf_op jit(solution)/shard_map/while
  400.0 12.6 %copy-start.15 = (bf16[128,576]{1,0:T(8,128)(2,1)S(1)}, bf16[128,576]{1,0:T(8,128)(2,1)}, u32[]{:S(2)}) copy-start(bf16[128,576]{1,0:T(8,128)(2,1)} %get-tuple-element.737) | copy-start | bytes 442372 | tf_op jit(solution)/shard_map/while
  400.0 12.6 %copy-start.17 = (bf16[128,544]{1,0:T(8,128)(2,1)S(1)}, bf16[128,544]{1,0:T(8,128)(2,1)}, u32[]{:S(2)}) copy-start(bf16[128,544]{1,0:T(8,128)(2,1)} %get-tuple-element.736) | copy-start | bytes 417796 | tf_op jit(solution)/shard_map/while
  445.4 10.0 %copy-start.7 = (bf16[128,704]{1,0:T(8,128)(2,1)S(1)}, bf16[128,704]{1,0:T(8,128)(2,1)}, u32[]{:S(2)}) copy-start(bf16[128,704]{1,0:T(8,128)(2,1)} %get-tuple-element.729) | copy-start | bytes 540676 | tf_op jit(solution)/shard_map/while
  445.4 10.0 %copy-start.9 = (bf16[128,672]{1,0:T(8,128)(2,1)S(1)}, bf16[128,672]{1,0:T(8,128)(2,1)}, u32[]{:S(2)}) copy-start(bf16[128,672]{1,0:T(8,128)(2,1)} %get-tuple-element.728) | copy-start | bytes 516100 | tf_op jit(solution)/shard_map/while
  445.4 11.5 %copy-start.19 = (bf16[128,640]{1,0:T(8,128)(2,1)S(1)}, bf16[128,640]{1,0:T(8,128)(2,1)}, u32[]{:S(2)}) copy-start(bf16[128,640]{1,0:T(8,128)(2,1)} %get-tuple-element.733) | copy-start | bytes 491524 | tf_op jit(solution)/shard_map/while
  445.4 11.5 %copy-start.21 = (bf16[128,608]{1,0:T(8,128)(2,1)S(1)}, bf16[128,608]{1,0:T(8,128)(2,1)}, u32[]{:S(2)}) copy-start(bf16[128,608]{1,0:T(8,128)(2,1)} %get-tuple-element.732) | copy-start | bytes 466948 | tf_op jit(solution)/shard_map/while
  445.7 12.6 %copy-start.15 = (bf16[128,576]{1,0:T(8,128)(2,1)S(1)}, bf16[128,576]{1,0:T(8,128)(2,1)}, u32[]{:S(2)}) copy-start(bf16[128,576]{1,0:T(8,128)(2,1)} %get-tuple-element.737) | copy-start | bytes 442372 | tf_op jit(solution)/shard_map/while
  445.7 12.6 %copy-start.17 = (bf16[128,544]{1,0:T(8,128)(2,1)S(1)}, bf16[128,544]{1,0:T(8,128)(2,1)}, u32[]{:S(2)}) copy-start(bf16[128,544]{1,0:T(8,128)(2,1)} %get-tuple-element.736) | copy-start | bytes 417796 | tf_op jit(solution)/shard_map/while
  491.1 10.0 %copy-start.7 = (bf16[128,704]{1,0:T(8,128)(2,1)S(1)}, bf16[128,704]{1,0:T(8,128)(2,1)}, u32[]{:S(2)}) copy-start(bf16[128,704]{1,0:T(8,128)(2,1)} %get-tuple-element.729) | copy-start | bytes 540676 | tf_op jit(solution)/shard_map/while
  491.1 10.0 %copy-start.9 = (bf16[128,672]{1,0:T(8,128)(2,1)S(1)}, bf16[128,672]{1,0:T(8,128)(2,1)}, u32[]{:S(2)}) copy-start(bf16[128,672]{1,0:T(8,128)(2,1)} %get-tuple-element.728) | copy-start | bytes 516100 | tf_op jit(solution)/shard_map/while
  491.1 11.5 %copy-start.19 = (bf16[128,640]{1,0:T(8,128)(2,1)S(1)}, bf16[128,640]{1,0:T(8,128)(2,1)}, u32[]{:S(2)}) copy-start(bf16[128,640]{1,0:T(8,128)(2,1)} %get-tuple-element.733) | copy-start | bytes 491524 | tf_op jit(solution)/shard_map/while
  491.1 11.5 %copy-start.21 = (bf16[128,608]{1,0:T(8,128)(2,1)S(1)}, bf16[128,608]{1,0:T(8,128)(2,1)}, u32[]{:S(2)}) copy-start(bf16[128,608]{1,0:T(8,128)(2,1)} %get-tuple-element.732) | copy-start | bytes 466948 | tf_op jit(solution)/shard_map/while
  491.4 12.6 %copy-start.15 = (bf16[128,576]{1,0:T(8,128)(2,1)S(1)}, bf16[128,576]{1,0:T(8,128)(2,1)}, u32[]{:S(2)}) copy-start(bf16[128,576]{1,0:T(8,128)(2,1)} %get-tuple-element.737) | copy-start | bytes 442372 | tf_op jit(solution)/shard_map/while
  491.5 12.6 %copy-start.17 = (bf16[128,544]{1,0:T(8,128)(2,1)S(1)}, bf16[128,544]{1,0:T(8,128)(2,1)}, u32[]{:S(2)}) copy-start(bf16[128,544]{1,0:T(8,128)(2,1)} %get-tuple-element.736) | copy-start | bytes 417796 | tf_op jit(solution)/shard_map/while
  (28 other events, 209.8 us)
Sparse Core Ops, SparseCore 0:
  39.3 14.3 all-gather.2
  259.3 10.2 all-gather.4
